TPU v7x, 8 devices: a whole 2x2x1 slice. The times are simulated.
8 devices in a mesh: dp: 1 (over z), pp: 2 (over y), ep: 4 (over x, core).
Axes of the slice: x: 2, y: 2, z: 1, core: 2. Of those that a mesh axis runs over, the one named last changes fastest.
Arguments:
- hidden_in: bfloat16 [64, 128, 1024], P(None, ('dp', 'ep'))
- seq_pos: int32 [64, 128], P(None, ('dp', 'ep'))
- k_cache: bfloat16 [2, 64, 128, 16, 8, 64], P('pp', None, ('dp', 'ep'))
- v_cache: bfloat16 [2, 64, 128, 16, 8, 64], P('pp', None, ('dp', 'ep'))
- expert_ids: int32 [2, 64, 128, 8], P('pp', None, ('dp', 'ep'))
- w_query: bfloat16 [2, 1024, 1024], P('pp')
- w_key: bfloat16 [2, 1024, 512], P('pp')
- w_value: bfloat16 [2, 1024, 512], P('pp')
- w_out: bfloat16 [2, 1024, 1024], P('pp')
- attn_gain: bfloat16 [2, 1024], P('pp')
- mlp_gain: bfloat16 [2, 1024], P('pp')
- w_router: bfloat16 [2, 1024, 32], P('pp')
- w_gate: bfloat16 [2, 32, 1024, 512], P('pp', 'ep')
- w_up: bfloat16 [2, 32, 1024, 512], P('pp', 'ep')
- w_down: bfloat16 [2, 32, 512, 1024], P('pp', 'ep')
- final_gain: bfloat16 [1024], replicated
Outputs:
- output 1: bfloat16 [64, 128, 1024], P(None, ('dp', 'ep'))
- output 2: bfloat16 [2, 64, 128, 8, 64], P('pp', None, ('dp', 'ep'))
- output 3: bfloat16 [2, 64, 128, 8, 64], P('pp', None, ('dp', 'ep'))
All inputs are finite; a program needn't handle non-finite values.
Results may differ from a plain program's by a relative error of at most 0.0174593.
Values are sent between devices in bfloat16 or wider.
A program may use at most 1 GiB of HBM per device.

v0:
```python
import functools

import jax
import jax.numpy as jnp
import numpy as np
from jax import lax
from jax.experimental import pallas as pl
from jax.experimental.pallas import tpu as pltpu
from jax.sharding import PartitionSpec as P

THETA = 1000000.0
EPS = 1e-05
F32 = jnp.float32
BF16 = jnp.bfloat16
TILE = 128
GROUP = 16
TILE_UNROLL = 3
PER_CHUNK = 4
HIN_SLOTS = 4
PIECES = 4
MESH = pl.DeviceIdType.MESH


def scope(name):
    return jax.named_scope(name)


def rms(vals, gain_row):
    inv = lax.rsqrt(jnp.mean(vals * vals, axis=-1, keepdims=True) + EPS)
    return (vals * inv * gain_row).astype(BF16)


def dot(lhs, rhs):
    return jnp.dot(lhs, rhs, preferred_element_type=F32)


def dot_nt(lhs, rhs):
    return lax.dot_general(lhs, rhs, (((1,), (1,)), ((), ())), preferred_element_type=F32)


def rope_tables(pos, table):
    lane = lax.broadcasted_iota(jnp.int32, pos.shape, 1).astype(F32)
    both = dot(jnp.where(lane + 1.0 == pos, 1.0, 0.0).astype(BF16), table[...])
    both = both[:, :256] + both[:, 256:512] + both[:, 512:]
    return both


def rope(vals, cos_t, sin_t):
    lane = lax.broadcasted_iota(jnp.int32, (1, 128), 1)
    first = (lane % 64) < 32
    parts = []
    for j in range(vals.shape[1] // 128):
        block = vals[:, j * 128:(j + 1) * 128]
        swapped = jnp.where(first, pltpu.roll(block, 96, 1), pltpu.roll(block, 32, 1))
        parts.append(block * cos_t + swapped * sin_t)
    return jnp.concatenate(parts, axis=1)


def spread(ref, vals):
    tokens = vals.shape[0]
    for g in range(8):
        ref[pl.ds(g, tokens, stride=8), :] = vals[:, g * 128:(g + 1) * 128]


def spread_heads(ref, vals):
    tokens = vals.shape[0]
    low = lax.broadcasted_iota(jnp.int32, (1, 128), 1) < 64
    for j in range(4):
        block = vals[:, j * 128:(j + 1) * 128]
        other = pltpu.roll(block, 64, 1)
        ref[pl.ds(2 * j, tokens, stride=8), :] = jnp.where(low, block, other)
        ref[pl.ds(2 * j + 1, tokens, stride=8), :] = jnp.where(low, other, block)


def rows_of(ref, idx):
    return ref[pl.ds(pl.multiple_of(idx * GROUP * 8, GROUP * 8), GROUP * 8), :].reshape(GROUP, 8, 128)


def attn_dots(hidden, w, raw):
    normed = rms(hidden.astype(F32), w["a_gain"][...].astype(F32))
    raw[1] = dot(normed, w["q"][...]).astype(BF16)
    raw[2, :, :512] = dot(normed, w["k"][...]).astype(BF16)
    raw[2, :, 512:] = dot(normed, w["v"][...]).astype(BF16)


def attn_rope(turn, raw, q3, k3, v3, kn, vn):
    cos_t, sin_t = turn[:, :128], turn[:, 128:]
    spread(q3, rope(raw[1].astype(F32), cos_t, sin_t).astype(BF16).astype(F32))
    k = rope(raw[2, :, :512].astype(F32), cos_t, sin_t).astype(BF16)
    kn[...] = k
    spread_heads(k3, k.astype(F32))
    v = raw[2, :, 512:]
    vn[...] = v
    spread_heads(v3, v.astype(F32))


def attn_scores(idx, q3, k3, k_rows):
    q = rows_of(q3, idx)
    lane3 = lax.broadcasted_iota(jnp.int32, (1, 1, 128), 2)
    prod = q * rows_of(k3, idx)
    self_a = jnp.sum(jnp.where(lane3 < 64, prod, 0.0), axis=-1, keepdims=True)
    self_b = jnp.sum(jnp.where(lane3 < 64, 0.0, prod), axis=-1, keepdims=True)
    wide = (GROUP, 8, 128)
    self_s = jnp.concatenate([jnp.broadcast_to(self_a, wide), jnp.broadcast_to(self_b, wide)], axis=1) * 0.125
    q_rows = jnp.concatenate([q, pltpu.roll(q, 64, 2)], axis=1).astype(BF16)[:, :, :64].reshape(GROUP * 16, 64)
    row0 = idx * (GROUP * 128)
    blocks = []
    for p in range(GROUP // 2):
        keys = k_rows[pl.ds(pl.multiple_of(row0 + p * 256, 256), 256), :]
        both = dot_nt(q_rows[p * 32:(p + 1) * 32], keys)
        blocks.append(both[:16, :128].reshape(1, 16, 128))
        blocks.append(both[16:, 128:].reshape(1, 16, 128))
    return jnp.concatenate(blocks, axis=0), self_s


def attn_weights(idx, scores, self_s, pos_ref):
    row_i = lax.broadcasted_iota(jnp.int32, (16, 128), 0)
    lane_i = lax.broadcasted_iota(jnp.int32, (16, 128), 1)
    step = jnp.where((row_i % 8) == (lane_i % 8), lane_i // 8, 1000).astype(F32)
    pos = pos_ref[pl.ds(pl.multiple_of(idx * GROUP, GROUP), GROUP), :].reshape(GROUP, 1, 128)
    scores = jnp.where(step.reshape(1, 16, 128) < pos, scores * 0.125, -jnp.inf)
    wide = (GROUP, 16, 128)
    top = jnp.maximum(jnp.broadcast_to(jnp.max(scores, axis=-1, keepdims=True), wide), self_s)
    weights = jnp.exp(scores - top)
    self_w = jnp.exp(self_s - top)
    inv = 1.0 / (jnp.broadcast_to(jnp.sum(weights, axis=-1, keepdims=True), wide) + self_w)
    return (weights * inv).astype(BF16), (self_w * inv).astype(BF16).astype(F32)


def attn_mix(idx, weights, self_w, v3, o3, v_rows):
    row0 = idx * (GROUP * 128)
    zeros = jnp.zeros((16, 128), BF16)
    outs = []
    for p in range(GROUP // 2):
        vals = v_rows[pl.ds(pl.multiple_of(row0 + p * 256, 256), 256), :]
        upper = jnp.concatenate([weights[2 * p], zeros], axis=1)
        lower = jnp.concatenate([zeros, weights[2 * p + 1]], axis=1)
        outs.append(dot(jnp.concatenate([upper, lower], axis=0), vals).reshape(2, 16, 64))
    out = jnp.concatenate(outs, axis=0)
    v_new = rows_of(v3, idx)[:, :, :64]
    out_a = out[:, :8] + self_w[:, :8, :64] * v_new
    out_b = out[:, 8:] + self_w[:, 8:, :64] * v_new
    o3[pl.ds(pl.multiple_of(idx * GROUP * 8, GROUP * 8), GROUP * 8), :] = jnp.concatenate([out_a, out_b], axis=-1).reshape(GROUP * 8, 128)


def plan_tiles(ids, first, tri, member_ref, rank_ref, table_ref):
    tokens = ids.shape[1]
    expert_i = lax.broadcasted_iota(jnp.int32, (32, tokens), 0)
    chosen = jnp.zeros((32, tokens), F32)
    for s in range(ids.shape[0]):
        chosen = jnp.where(ids[s:s + 1, :] == expert_i, 1.0, chosen)
    member_ref[...] = chosen
    rank = dot(chosen.astype(BF16), tri[...])
    rank_ref[...] = jnp.where(chosen > 0.0, rank, -1.0)
    local = member_ref[pl.ds(pl.multiple_of(first, 8), 8), :]
    counts = jnp.sum(local, axis=-1, keepdims=True).astype(jnp.int32)
    tiles = jnp.broadcast_to(lax.shift_right_logical(counts + (TILE - 1), 7), (8, 128))
    lane = lax.broadcasted_iota(jnp.int32, (1, 128), 1)
    end = jnp.zeros((1, 128), jnp.int32)
    start = jnp.zeros((1, 128), jnp.int32)
    expert = jnp.zeros((1, 128), jnp.int32)
    for e in range(8):
        end = end + tiles[e:e + 1, :]
        passed = lane >= end
        expert = jnp.where(passed, expert + 1, expert)
        start = jnp.where(passed, end, start)
    sub = jnp.where(expert < 8, lane - start, 1000)
    table_ref[0:1, :] = jnp.minimum(expert, 7)
    table_ref[1:2, :] = sub


def moe_gates(logits, rank_ref, gate_ref):
    chosen = rank_ref[...] >= 0.0
    top = jnp.max(jnp.where(chosen, logits, -jnp.inf), axis=0, keepdims=True)
    gates = jnp.where(chosen, jnp.exp(logits - top), 0.0)
    gate_ref[...] = gates / jnp.sum(gates, axis=0, keepdims=True)


def slot_of(u):
    return 0 if u == 0 else 1 + (u - 1) % 2


def moe_gather(j, u, expert, sub, first, normed, rank_ref, picks, x_buf):
    ranks = rank_ref[pl.ds(first + expert, 1), :]
    wanted = (lax.broadcasted_iota(jnp.int32, (TILE, 1), 0) + sub * TILE).astype(F32)
    picked = jnp.where(ranks == wanted, 1.0, 0.0)
    picks[:, pl.ds(pl.multiple_of(j * TILE, TILE), TILE)] = picked.T.astype(BF16)
    x_buf[slot_of(u)] = dot(picked.astype(BF16), normed[...]).astype(BF16)
    return picked


def moe_gate(picked, u, expert, first, gate_ref, g_buf):
    gate = jnp.sum(picked * gate_ref[pl.ds(first + expert, 1), :], axis=-1, keepdims=True)
    g_buf[u] = jnp.broadcast_to(gate, (TILE, 128))


def moe_expand(u, expert, w, x_buf, a_buf):
    rows = x_buf[slot_of(u)]
    a_buf[slot_of(u)] = (jax.nn.silu(dot(rows, w["gate"][expert])) * dot(rows, w["up"][expert])).astype(BF16)


def moe_contract(j, u, expert, w, a_buf, g_buf, terms):
    y = dot(a_buf[slot_of(u)], w["down"][expert])
    gate = g_buf[u]
    at = pl.ds(pl.multiple_of(j * TILE, TILE), TILE)
    for p in range(8):
        terms[at, p * 128:(p + 1) * 128] = (gate * y[:, p * 128:(p + 1) * 128]).astype(BF16)


def step_kernel(
    tile_count,
    hid, seq, k_cache, v_cache, ids_own, wq_h, wk_h, wv_h, wo_h, a_gain, m_gain, rope_ref, w_r, wg_h, wu_h, wd_h, tri,
    out, kn_out, vn_out,
    n_buf, hin, mid, ho, k_buf, v_buf, wq, wk, wv, wo, wg, wu, wd, part, rb1, rb2, picks, terms, x_buf, a_buf, g_buf, q3, k3, v3, o3, kn, vn, rank_buf, gate_ref, member, pos, turn, ids, table, smem_table,
    w_sem, ids_send, ids_recv, table_sem, hin_sem, kv_sem, new_sem, dx_send, dx_recv, dc_send, dc_recv, dr_send, dr_recv, r1_send, r1_recv, r2_send, r2_recv, hop_send, out_loc, out_recv, credit,
):
    chunks, tokens = hid.shape[0], hid.shape[1]
    gathered = 4 * tokens
    dp = lax.axis_index("dp")
    pp = lax.axis_index("pp")
    ep = lax.axis_index("ep")
    other_pp = (dp, 1 - pp, ep)
    across = (dp, pp, lax.rem(ep + 2, 4))
    beside = (dp, pp, ep + 1 - 2 * lax.rem(ep, 2))
    first = ep * 8

    diagonal = (dp, pp, lax.rem(ep + 3 - 2 * lax.rem(ep, 2), 4))

    attn_w = [(wq_h, wq), (wk_h, wk), (wv_h, wv), (wo_h, wo)]
    moe_w = [(wg_h, wg), (wu_h, wu), (wd_h, wd)]
    weight_copies = [pltpu.make_async_copy(s, d, w_sem.at[j]) for j, (s, d) in enumerate(attn_w + moe_w)]

    def hin_copies(c):
        h = lax.rem(c, HIN_SLOTS)
        return [pltpu.make_async_copy(hid.at[c, piece(p)], hin.at[h, piece(p)], hin_sem.at[h, p]) for p in range(PIECES)]

    def kv_copies(c):
        return (pltpu.make_async_copy(k_cache.at[c], k_buf, kv_sem.at[0]), pltpu.make_async_copy(v_cache.at[c], v_buf, kv_sem.at[1]))

    def new_copies(c):
        return (pltpu.make_async_copy(kn, kn_out.at[c], new_sem.at[0]), pltpu.make_async_copy(vn, vn_out.at[c], new_sem.at[1]))

    def remote(src, dst, send, recv, peer):
        return pltpu.make_async_remote_copy(src_ref=src, dst_ref=dst, send_sem=send, recv_sem=recv, device_id=peer, device_id_type=MESH)

    def rows_at(slot, part_idx):
        return n_buf.at[slot, pl.ds(part_idx * tokens, tokens)]

    def dx_copy(c):
        s = lax.rem(c, 3)
        return remote(rows_at(s, 0), rows_at(s, 1), dx_send.at[s], dx_recv.at[s], across)

    def dc_copy(c):
        s = lax.rem(c, 3)
        return remote(rows_at(s, 0), rows_at(s, 2), dc_send.at[s], dc_recv.at[s], beside)

    def dr_copy(c):
        s = lax.rem(c, 3)
        return remote(rows_at(s, 1), rows_at(s, 3), dr_send.at[s], dr_recv.at[s], beside)

    def r1_copy(c, home):
        s = lax.rem(c, 2)
        return remote(part.at[pl.ds((2 + home) * tokens, tokens)], rb1.at[s, pl.ds(home * tokens, tokens)], r1_send.at[s, home], r1_recv.at[s, home], beside)

    rows = tokens // PIECES

    def piece(p):
        return pl.ds(pl.multiple_of(p * rows, rows), rows)

    def r2_copy(c, p):
        s = lax.rem(c, 3)
        return remote(rb1.at[lax.rem(c, 2), pl.ds(tokens + p * rows, rows)], rb2.at[s, piece(p)], r2_send.at[s, p], r2_recv.at[s, p], across)

    def hop_copy(c, p):
        s = lax.rem(c, 2)
        h = lax.rem(c, HIN_SLOTS)
        return remote(ho.at[s, piece(p)], hin.at[h, piece(p)], hop_send.at[s, p], hin_sem.at[h, p], other_pp)

    def out_copy(c, p):
        s = lax.rem(c, 2)
        return remote(ho.at[s, piece(p)], out.at[c, piece(p)], hop_send.at[s, p], out_recv.at[c, p], other_pp)

    def out_local(c, p):
        s = lax.rem(c, 2)
        return pltpu.make_async_copy(ho.at[s, piece(p)], out.at[c, piece(p)], out_loc.at[s, p])

    def ids_copies(part_idx):
        some = pl.ds(0, 1) if part_idx == 0 else pl.ds(1, chunks - 1)
        return [remote(ids_own.at[some], ids.at[j, some], ids_send.at[part_idx, j], ids_recv.at[part_idx, j], peer) for j, peer in ((1, across), (2, beside), (3, diagonal))]

    def table_copy(c):
        s = lax.rem(c, 2)
        return pltpu.make_async_copy(table, smem_table.at[s], table_sem)

    smem_table[1, 0, 0] = 0
    smem_table[1, 1, 0] = 0

    @pl.when(pp == 0)
    def _():
        for copy in hin_copies(0):
            copy.start()

    for copy in weight_copies[:3]:
        copy.start()
    for copy in kv_copies(0):
        copy.start()
    weight_copies[3].start()

    @pl.when(pp == 0)
    def _():
        for copy in hin_copies(1):
            copy.start()

    barrier = pltpu.get_barrier_semaphore()
    for peer in (other_pp, across, beside, diagonal):
        pl.semaphore_signal(barrier, inc=1, device_id=peer, device_id_type=MESH)
    pl.semaphore_wait(barrier, 4)

    for part_idx in range(2):
        for copy in ids_copies(part_idx):
            copy.start()

    w = {"a_gain": a_gain, "rope": rope_ref, "q": wq, "k": wk, "v": wv, "gate": wg, "up": wu, "down": wd}

    def plan(c):
        @pl.when(c == 0)
        def _():
            ids[0] = ids_own[...]
            with scope("w_ids"):
                for copy in ids_copies(0):
                    copy.wait()

        @pl.when(c == 1)
        def _():
            for copy in ids_copies(1):
                copy.wait()

        chosen_ids = jnp.concatenate([ids[j, c] for j in range(4)], axis=1)
        plan_tiles(chosen_ids, first, tri, member, rank_buf.at[lax.rem(c, 2)], table)
        table_copy(c).start()

    def combine_near(from_col, to_col):
        half = pl.ds(0, 2 * tokens)
        part[half, from_col:to_col] = dot(picks[half, :], terms[:, from_col:to_col])

    def project(c, with_sums):
        plan(c)
        with scope("w_hin"):
            for copy in hin_copies(c):
                copy.wait()

        @pl.when(c == 0)
        def _():
            for copy in weight_copies[:3]:
                copy.wait()

        @pl.when(jnp.logical_and(pp == 0, c + 2 < chunks))
        def _():
            for copy in hin_copies(c + 2):
                copy.start()

        @pl.when(c > 0)
        def _():
            for copy in new_copies(c - 1):
                copy.wait()

        seq_row = seq[pl.ds(c, 1), :].astype(F32)
        pos[...] = jnp.broadcast_to(seq_row, (128, 128)).T
        turn[...] = rope_tables(pos[...], w["rope"])
        if with_sums:
            combine_near(0, 256)
        attn_dots(hin[lax.rem(c, HIN_SLOTS)], w, x_buf)
        if with_sums:
            combine_near(256, 1024)
        attn_rope(turn, x_buf, q3, k3, v3, kn, vn)
        for copy in new_copies(c):
            copy.start()

    def reduce_pair(c):
        s = lax.rem(c, 2)
        far = pl.ds(tokens, tokens)
        near = pl.ds(0, tokens)
        with scope("w_r1"):
            r1_copy(c, 1).wait_recv()
        rb1[s, far, :] = rb1[s, far, :] + part[far, :]
        for p in range(PIECES):
            r2_copy(c, p).start()
        r1_copy(c, 0).wait_recv()
        rb1[s, near, :] = rb1[s, near, :] + part[near, :]
        for home in (1, 0):
            r1_copy(c, home).wait_send()

    def relay(c):
        copy = dx_copy(c)
        with scope("w_dx"):
            copy.wait_recv()
        dr_copy(c).start()
        copy.wait_send()
        dc_copy(c).wait_send()

    def attend(c):
        table_copy(c).wait()
        with scope("w_kv"):
            for copy in kv_copies(c):
                copy.wait()

        @pl.when(c == 0)
        def _():
            weight_copies[4].start()

        @pl.when(c == 1 - pp)
        def _():
            for copy in weight_copies[5:]:
                copy.start()

        def groups(base, count):
            ahead = attn_scores(base, q3, k3, k_buf)
            for u in range(base, base + count):
                scores = ahead
                if u + 1 < base + count:
                    ahead = attn_scores(u + 1, q3, k3, k_buf)
                attn_mix(u, *attn_weights(u, *scores, pos), v3, o3, v_buf)

        half = tokens // GROUP // 2
        with scope("groups"):
            groups(0, half)

        @pl.when(c >= 2)
        def _():
            with scope("relay"):
                relay(c - 1)

        with scope("groups"):
            groups(half, half)

        @pl.when(c + 1 < chunks)
        def _():
            for copy in kv_copies(c + 1):
                copy.start()

        @pl.when(c == 0)
        def _():
            weight_copies[3].wait()

        @pl.when(c == 1)
        def _():
            relay(0)

        @pl.when(c >= 1)
        def _():
            dispatched(c - 1)

        hidden = hin[lax.rem(c, HIN_SLOTS)].astype(F32)
        attn_out = jnp.concatenate([o3[pl.ds(g, tokens, stride=8), :].astype(BF16) for g in range(8)], axis=1)
        before = c + 5
        mixed = dot(attn_out, wo[...])
        router = logits(before)
        picked = gather_rows(before, 0, 0)
        new_mid = (hidden + mixed).astype(BF16)
        mid[lax.rem(c, 3)] = new_mid
        n_buf[lax.rem(c, 3), pl.ds(0, tokens), :] = rms(new_mid.astype(F32), m_gain[...].astype(F32))
        gates(before, router)
        gather_gate(picked, before, 0, 0)
        dx_copy(c).start()
        dc_copy(c).start()

        @pl.when(jnp.logical_and(pp == 1, c + HIN_SLOTS < chunks))
        def _():
            pl.semaphore_signal(credit, inc=1, device_id=other_pp, device_id_type=MESH)

    def tile_at(c, row, j):
        return smem_table[lax.rem(c, 2), row, j]

    def gather_rows(c, j, u):
        normed = n_buf.at[lax.rem(c, 3)]
        return moe_gather(j, u, tile_at(c, 0, j), tile_at(c, 1, j), first, normed, rank_buf.at[lax.rem(c, 2)], picks, x_buf)

    def gather_gate(picked, c, j, u):
        moe_gate(picked, u, tile_at(c, 0, j), first, gate_ref, g_buf)

    def gather(c, j, u):
        gather_gate(gather_rows(c, j, u), c, j, u)

    def dispatched(c):
        with scope("w_disp"):
            dc_copy(c).wait_recv()
            dr_copy(c).wait_recv()

    def logits(c):
        return dot_nt(w_r[...], n_buf[lax.rem(c, 3)])

    def gates(c, router):
        moe_gates(router, rank_buf.at[lax.rem(c, 2)], gate_ref)

    def experts(c):
        @pl.when(c == 0)
        def _():
            with scope("w_wts"):
                for copy in weight_copies[4:]:
                    copy.wait()

        def expand(j, u):
            moe_expand(u, tile_at(c, 0, j), w, x_buf, a_buf)

        def contract(j, u):
            moe_contract(j, u, tile_at(c, 0, j), w, a_buf, g_buf, terms)

        def body(idx, carry):
            base = idx * TILE_UNROLL
            gather(c, base + 1, 1)
            expand(base, 0)
            for u in range(1, TILE_UNROLL):
                if u + 1 < TILE_UNROLL:
                    gather(c, base + u + 1, u + 1)
                expand(base + u, u)
                contract(base + u - 1, u - 1)
            gather(c, lax.rem(base + TILE_UNROLL, tile_count), 0)
            contract(base + TILE_UNROLL - 1, TILE_UNROLL - 1)

            @pl.when(jnp.logical_and(c >= 1, idx >= 1))
            def _():
                finish(c - 1, idx - 1)

            return carry

        with scope("tiles"):
            lax.fori_loop(0, tile_count // TILE_UNROLL, body, 0)
        half = 2 * tokens
        part[pl.ds(half, half), :] = dot(picks[pl.ds(half, half), :], terms[...])
        dr_copy(c).wait_send()
        r1_copy(c, 1).start()
        r1_copy(c, 0).start()

    def finish(c, p):
        s = lax.rem(c, 2)
        at = piece(p)

        @pl.when(jnp.logical_and(jnp.logical_and(pp == 0, p == 0), c >= HIN_SLOTS))
        def _():
            pl.semaphore_wait(credit, 1)

        @pl.when(jnp.logical_and(pp == 0, c >= 2))
        def _():
            hop_copy(c - 2, p).wait_send()

        @pl.when(jnp.logical_and(pp == 1, c >= 2))
        def _():
            out_copy(c - 2, p).wait_send()
            out_local(c - 2, p).wait()

        with scope("w_r2"):
            r2_copy(c, p).wait_recv()
            r2_copy(c, p).wait_send()
        mixed = (rb1[s, at, :] + rb2[lax.rem(c, 3), at, :]).astype(BF16)
        ho[s, at, :] = (mid[lax.rem(c, 3), at, :].astype(F32) + mixed.astype(F32)).astype(BF16)

        @pl.when(pp == 0)
        def _():
            hop_copy(c, p).start()

        @pl.when(pp == 1)
        def _():
            out_copy(c, p).start()
            out_local(c, p).start()

    def step(i, carry):
        @pl.when(i < 2)
        def _():
            with scope("project"):
                project(i, False)

        @pl.when(jnp.logical_and(i >= 2, i < chunks))
        def _():
            with scope("project_sum"):
                project(i, True)

        @pl.when(i >= chunks)
        def _():
            combine_near(0, 1024)

        @pl.when(i >= 2)
        def _():
            with scope("reduce_pair"):
                reduce_pair(i - 2)

        @pl.when(i == chunks)
        def _():
            with scope("relay"):
                relay(i - 1)

        @pl.when(i < chunks)
        def _():
            with scope("attend"):
                attend(i)

        @pl.when(i == chunks)
        def _():
            dispatched(i - 1)
            gates(i - 1, logits(i - 1))
            gather(i - 1, 0, 0)

        @pl.when(jnp.logical_and(i >= 1, i <= chunks))
        def _():
            with scope("experts"):
                experts(i - 1)

        @pl.when(i == chunks + 1)
        def _():
            with scope("finish_last"):
                for p in range(PIECES):
                    finish(i - 2, p)

        return carry

    lax.fori_loop(0, chunks + 2, step, 0)

    for copy in new_copies(chunks - 1):
        copy.wait()

    @pl.when(pp == 0)
    def _():
        for c in (chunks - 2, chunks - 1):
            for p in range(PIECES):
                hop_copy(c, p).wait_send()

        def arrived(c, carry):
            for p in range(PIECES):
                out_copy(c, p).wait_recv()
            return carry

        with scope("w_out"):
            lax.fori_loop(0, chunks, arrived, 0)

    @pl.when(pp == 1)
    def _():
        for c in (chunks - 2, chunks - 1):
            for p in range(PIECES):
                out_copy(c, p).wait_send()
                out_local(c, p).wait()


def step_call(args, chunks, tokens, tile_count):
    vmem = pl.BlockSpec(memory_space=pltpu.VMEM)
    hbm = pl.BlockSpec(memory_space=pl.ANY)
    wide = 4 * tokens
    dma = pltpu.SemaphoreType.DMA
    return pl.pallas_call(
        functools.partial(step_kernel, tile_count),
        out_shape=(
            jax.ShapeDtypeStruct((chunks, tokens, 1024), BF16),
            jax.ShapeDtypeStruct((chunks, tokens, 512), BF16),
            jax.ShapeDtypeStruct((chunks, tokens, 512), BF16),
        ),
        in_specs=[hbm, vmem, hbm, hbm, vmem, hbm, hbm, hbm, hbm, vmem, vmem, vmem, vmem, hbm, hbm, hbm, vmem],
        out_specs=(hbm, hbm, hbm),
        scratch_shapes=[
            pltpu.VMEM((3, wide, 1024), BF16),
            pltpu.VMEM((HIN_SLOTS, tokens, 1024), BF16),
            pltpu.VMEM((3, tokens, 1024), BF16),
            pltpu.VMEM((2, tokens, 1024), BF16),
            pltpu.VMEM((tokens * 128, 64), BF16),
            pltpu.VMEM((tokens * 128, 64), BF16),
            pltpu.VMEM((1024, 1024), BF16),
            pltpu.VMEM((1024, 512), BF16),
            pltpu.VMEM((1024, 512), BF16),
            pltpu.VMEM((1024, 1024), BF16),
            pltpu.VMEM((8, 1024, 512), BF16),
            pltpu.VMEM((8, 1024, 512), BF16),
            pltpu.VMEM((8, 512, 1024), BF16),
            pltpu.VMEM((wide, 1024), F32),
            pltpu.VMEM((2, 2 * tokens, 1024), F32),
            pltpu.VMEM((3, tokens, 1024), F32),
            pltpu.VMEM((wide, tile_count * TILE), BF16),
            pltpu.VMEM((tile_count * TILE, 1024), BF16),
            pltpu.VMEM((3, TILE, 1024), BF16),
            pltpu.VMEM((3, TILE, 512), BF16),
            pltpu.VMEM((TILE_UNROLL, TILE, 128), F32),
            pltpu.VMEM((tokens * 8, 128), F32),
            pltpu.VMEM((tokens * 8, 128), F32),
            pltpu.VMEM((tokens * 8, 128), F32),
            pltpu.VMEM((tokens * 8, 128), F32),
            pltpu.VMEM((tokens, 512), BF16),
            pltpu.VMEM((tokens, 512), BF16),
            pltpu.VMEM((2, 32, wide), F32),
            pltpu.VMEM((32, wide), F32),
            pltpu.VMEM((32, wide), F32),
            pltpu.VMEM((tokens, 128), F32),
            pltpu.VMEM((tokens, 256), F32),
            pltpu.VMEM((4, chunks, 8, tokens), jnp.int32),
            pltpu.VMEM((8, 128), jnp.int32),
            pltpu.SMEM((2, 8, 128), jnp.int32),
            dma((7,)), dma((2, 4)), dma((2, 4)), dma(()), dma((HIN_SLOTS, PIECES)), dma((2,)), dma((2,)),
            dma((3,)), dma((3,)), dma((3,)), dma((3,)), dma((3,)), dma((3,)),
            dma((2, 2)), dma((2, 2)), dma((3, PIECES)), dma((3, PIECES)),
            dma((2, PIECES)), dma((2, PIECES)), dma((chunks, PIECES)),
            pltpu.SemaphoreType.REGULAR,
        ],
        compiler_params=pltpu.CompilerParams(collective_id=0, has_side_effects=True, vmem_limit_bytes=67043328),
        name="decode_step",
        cost_estimate=pl.CostEstimate(flops=2 * 10**11, bytes_accessed=2 * 10**8, transcendentals=0),
    )(*args)


def result_kernel(h_ref, k_ref, v_ref, gain_ref, out_ref, kn_ref, vn_ref, rows):
    tokens = rows.shape[1] // 8
    gain = gain_ref[...].astype(F32).reshape(1, 1024)

    def body(idx, carry):
        at = pl.ds(pl.multiple_of(idx * tokens, tokens), tokens)
        vals = h_ref[0, at, :].astype(F32)
        vals = vals * lax.rsqrt(jnp.mean(vals * vals, axis=-1, keepdims=True) + EPS)
        for g in range(8):
            out_ref[0, at, g * 128:(g + 1) * 128] = (vals[:, g * 128:(g + 1) * 128] * gain[:, g * 128:(g + 1) * 128]).astype(BF16)
        for j, (src, dst) in enumerate(((k_ref, kn_ref), (v_ref, vn_ref))):
            spread_heads(rows.at[j], src[0, at, :].astype(F32))
            dst[0, at] = rows[j].reshape(tokens, 8, 128)[:, :, :64].astype(BF16)
        return carry

    lax.fori_loop(0, h_ref.shape[1] // tokens, body, 0)


def result_call(hidden, k_rows, v_rows, gain):
    blocks = 4
    step = hidden.shape[1]
    tokens = hidden.shape[0] * step // blocks
    hidden, k_rows, v_rows = (x.reshape(blocks, tokens, x.shape[-1]) for x in (hidden, k_rows, v_rows))
    chunks = blocks
    wide = pl.BlockSpec((1, tokens, 1024), lambda i: (i, 0, 0))
    dense = pl.BlockSpec((1, tokens, 512), lambda i: (i, 0, 0))
    heads = pl.BlockSpec((1, tokens, 8, 64), lambda i: (i, 0, 0, 0))
    return pl.pallas_call(
        result_kernel,
        grid=(chunks,),
        out_shape=(
            jax.ShapeDtypeStruct((chunks, tokens, 1024), BF16),
            jax.ShapeDtypeStruct((chunks, tokens, 8, 64), BF16),
            jax.ShapeDtypeStruct((chunks, tokens, 8, 64), BF16),
        ),
        in_specs=[wide, dense, dense, pl.BlockSpec((1024,), lambda i: (0,))],
        out_specs=(wide, heads, heads),
        scratch_shapes=[pltpu.VMEM((2, step * 8, 128), F32)],
        name="results",
        cost_estimate=pl.CostEstimate(flops=10**7, bytes_accessed=2 * 10**7, transcendentals=0),
    )(hidden, k_rows, v_rows, gain)


def solution(mesh):
    rows_spec = ("dp", "ep")
    three_dim = P("pp", None, None)
    two_dim = P("pp", None)
    expert_spec = P("pp", "ep", None, None)
    cache_spec = P("pp", None, rows_spec, None, None, None)
    new_spec = P("pp", None, rows_spec, None, None)
    in_specs = (P(None, rows_spec, None), P(None, rows_spec), cache_spec, cache_spec, P("pp", None, rows_spec, None), three_dim, three_dim, three_dim, three_dim, two_dim, two_dim, three_dim, expert_spec, expert_spec, expert_spec, P(None))
    out_specs = (P(None, rows_spec, None), new_spec, new_spec)

    def device_fn(hidden_in, seq_pos, k_cache, v_cache, expert_ids, w_query, w_key, w_value, w_out, attn_gain, mlp_gain, w_router, w_gate, w_up, w_down, final_gain):
        micro, rows = seq_pos.shape
        chunks = micro // PER_CHUNK
        tokens = PER_CHUNK * rows
        wide = 4 * tokens
        tile_count = (wide * 2 - 8) // TILE + 8
        assert tile_count == TILE_UNROLL * (PIECES + 1)
        angles = np.arange(1, 17)[:, None] * THETA ** (-np.arange(32) / 32)
        both = np.concatenate([np.tile(np.cos(angles), (1, 4)), np.tile(np.concatenate([-np.sin(angles), np.sin(angles)], axis=1), (1, 2))], axis=1)
        both = np.concatenate([both, np.zeros((112, 256))], axis=0).astype(np.float32)
        table = []
        for _ in range(3):
            table.append(both.astype(BF16))
            both = both - table[-1].astype(np.float32)
        table = jnp.asarray(np.concatenate(table, axis=1))
        tri = jnp.asarray(np.triu(np.ones((wide, wide)), 1), BF16)
        ids = jnp.swapaxes(expert_ids[0].reshape(chunks, tokens, 8), 1, 2)
        args = (
            hidden_in.reshape(chunks, tokens, 1024), seq_pos.reshape(chunks, tokens), k_cache.reshape(chunks, tokens * 128, 64), v_cache.reshape(chunks, tokens * 128, 64),
            ids, w_query[0], w_key[0], w_value[0], w_out[0], attn_gain, mlp_gain, table, w_router[0].T,
            w_gate[0], w_up[0], w_down[0], tri,
        )
        out, k_new, v_new = result_call(*step_call(args, chunks, tokens, tile_count), final_gain)
        shape = (1,) + seq_pos.shape + (8, 64)
        return out.reshape(hidden_in.shape), k_new.reshape(shape), v_new.reshape(shape)

    return jax.shard_map(device_fn, mesh=mesh, in_specs=in_specs, out_specs=out_specs, check_vma=False)
```

profile of v0, /device:TPU:0, one launch (start us, length us, event | category | flops | bytes accessed | tf_op | source)
XLA Modules:
  0.0 386.7 jit_solution(1700527585666852019)
XLA Ops:
  0.6 0.8 copy.22
  1.4 0.7 reshape.37.seq
  2.1 1.0 copy.23
  3.1 0.1 reshape_squeeze.3
  3.3 0.7 copy.26
  3.9 371.5 %decode_step.1 = (bf16[16,128,1024]{2,1,0:T(8,128)(2,1)}, bf16[16,128,512]{2,1,0:T(8,128)(2,1)}, bf16[16,128,512]{2,1,0:T(8,128)(2,1)}) custom-call(bf16[16,128,1024]{2,1,0:T(8,128)(2,1)} %bitcast.33, s32[16,128]{1,0:T(8,128)} %reshape.37.seq, bf16[16,16384,64]{2,1,0:T(8,128)(2,1)} %bitcast.1.k_cache, bf16[16,16384,64]{2,1,0:T(8,128)(2,1)} %bitcast.2.v_cache, ...), custom_call_target="tpu_custom_call" | custom-call | flops 199999995904 | bytes 200000000 | tf_op jit(solution)/shard_map/decode_step/pallas_call | solution.py:647
  375.4 11.2 %results.1 = (bf16[4,512,1024]{2,1,0:T(8,128)(2,1)}, bf16[4,512,8,64]{3,2,1,0:T(8,128)(2,1)}, bf16[4,512,8,64]{3,2,1,0:T(8,128)(2,1)}) custom-call(bf16[4,512,1024]{2,1,0:T(8,128)(2,1)} %bitcast.26, bf16[4,512,512]{2,1,0:T(8,128)(2,1)} %bitcast.27, bf16[4,512,512]{2,1,0:T(8,128)(2,1)} %bitcast.28, bf16[1024]{0:T(1024)(128)(2,1)} %gain_ref.1), custom_call_target="tpu_custom_call" | custom-call | flops 10000000 | bytes 20000000 | tf_op jit(solution)/shard_map/results/pallas_call | solution.py:731
where the time goes:
time: 387 us
  Pallas kernels  383 us (99%)
    pallas_call x1, Pallas kernels, step_call(): pl.pallas_call(functools.partial(step_kernel, tile_count), out_shape=(jax...  372 us
    pallas_call x1, Pallas kernels, result_call(): pl.pallas_call(result_kernel, grid=(chunks,), out_shape=(jax.ShapeDtypeSt...  11.2 us

commit v1 on v0

--- a/solution.py
+++ b/solution.py
@@ -379,14 +379,12 @@
     def reduce_pair(c):
         s = lax.rem(c, 2)
         far = pl.ds(tokens, tokens)
-        near = pl.ds(0, tokens)
         with scope("w_r1"):
             r1_copy(c, 1).wait_recv()
         rb1[s, far, :] = rb1[s, far, :] + part[far, :]
         for p in range(PIECES):
             r2_copy(c, p).start()
         r1_copy(c, 0).wait_recv()
-        rb1[s, near, :] = rb1[s, near, :] + part[near, :]
         for home in (1, 0):
             r1_copy(c, home).wait_send()
 
@@ -551,7 +549,7 @@
         with scope("w_r2"):
             r2_copy(c, p).wait_recv()
             r2_copy(c, p).wait_send()
-        mixed = (rb1[s, at, :] + rb2[lax.rem(c, 3), at, :]).astype(BF16)
+        mixed = (rb1[s, at, :] + part[at, :] + rb2[lax.rem(c, 3), at, :]).astype(BF16)
         ho[s, at, :] = (mid[lax.rem(c, 3), at, :].astype(F32) + mixed.astype(F32)).astype(BF16)
 
         @pl.when(pp == 0)

time: 387 us -> 386 us (level)
  no operation moved by 1% of the time
where the time goes in v1:
time: 386 us
  Pallas kernels  382 us (99%)
    pallas_call x1, Pallas kernels, step_call(): pl.pallas_call(functools.partial(step_kernel, tile_count), out_shape=(jax...  371 us
    pallas_call x1, Pallas kernels, result_call(): pl.pallas_call(result_kernel, grid=(chunks,), out_shape=(jax.ShapeDtypeSt...  11.2 us

profile of v1, /device:TPU:0, one launch (start us, length us, event | category | flops | bytes accessed | tf_op | source)
XLA Modules:
  0.0 386.1 jit_solution(3286476810445227149)
XLA Ops:
  0.6 0.8 copy.22
  1.4 0.7 reshape.37.seq
  2.1 1.0 copy.23
  3.1 0.1 reshape_squeeze.3
  3.3 0.7 copy.26
  3.9 371.0 %decode_step.1 = (bf16[16,128,1024]{2,1,0:T(8,128)(2,1)}, bf16[16,128,512]{2,1,0:T(8,128)(2,1)}, bf16[16,128,512]{2,1,0:T(8,128)(2,1)}) custom-call(bf16[16,128,1024]{2,1,0:T(8,128)(2,1)} %bitcast.33, s32[16,128]{1,0:T(8,128)} %reshape.37.seq, bf16[16,16384,64]{2,1,0:T(8,128)(2,1)} %bitcast.1.k_cache, bf16[16,16384,64]{2,1,0:T(8,128)(2,1)} %bitcast.2.v_cache, ...), custom_call_target="tpu_custom_call" | custom-call | flops 199999995904 | bytes 200000000 | tf_op jit(solution)/shard_map/decode_step/pallas_call | solution.py:645
  374.9 11.2 %results.1 = (bf16[4,512,1024]{2,1,0:T(8,128)(2,1)}, bf16[4,512,8,64]{3,2,1,0:T(8,128)(2,1)}, bf16[4,512,8,64]{3,2,1,0:T(8,128)(2,1)}) custom-call(bf16[4,512,1024]{2,1,0:T(8,128)(2,1)} %bitcast.26, bf16[4,512,512]{2,1,0:T(8,128)(2,1)} %bitcast.27, bf16[4,512,512]{2,1,0:T(8,128)(2,1)} %bitcast.28, bf16[1024]{0:T(1024)(128)(2,1)} %gain_ref.1), custom_call_target="tpu_custom_call" | custom-call | flops 10000000 | bytes 20000000 | tf_op jit(solution)/shard_map/results/pallas_call | solution.py:729
